TPU v7x, 32 devices: a whole 2x2x4 slice. The times are simulated.
32 devices in a mesh: seq: 8 (over z, x), rows: 4 (over y, core).
Axes of the slice: x: 2, y: 2, z: 4, core: 2. Of those that a mesh axis runs over, the one named last changes fastest.
Arguments:
- attn_in: bfloat16 [8192, 8192], P(('seq', 'rows')), may hold values from -6 to 6
- attn_out: bfloat16 [8192, 8192], P(('seq', 'rows')), may hold values from -6 to 6
- valid: int32 [8192], P(('seq', 'rows')), may hold values 0 or 1
- w_qkv: bfloat16 [10240, 8192], P('rows', 'seq'), may hold values from -6 to 6
- w_out: bfloat16 [8192, 8192], P('rows', 'seq'), may hold values from -6 to 6
- qkv_ranks: int32 [10240], P('rows'), may hold values from 3072 to 5120
- out_ranks: int32 [8192], P('rows'), may hold values from 3072 to 5120
Outputs:
- qkv_margins: float32 [10240, 8192], P('rows', 'seq')
- out_margins: float32 [8192, 8192], P('rows', 'seq')
Inputs may be any that keep to these rules, and one draw needn't show every extreme that they name: `qkv_ranks`: each row keeps between three and five eighths of its 8192 weights. `out_ranks`: each row keeps between three and five eighths of its 8192 weights.
All inputs are finite; a program needn't handle non-finite values. No bound on the sum of `valid` on one device may be relied on, other than what follows from the above.
Results may differ from a plain program's by a relative error of at most 0.0003.
Values may be sent and summed in bfloat16 or wider, within the bound.
A program may use at most 128 MiB of HBM per device.

v0:
```python
import jax
import jax.numpy as jnp
from jax import lax
from jax.sharding import PartitionSpec as P

EPS = 1e-06


def tile_scores(weights, norm):
    return jnp.abs(weights.astype(jnp.float32)) * norm[None, :]


def row_limits(scores, ranks):
    lower = jnp.zeros((scores.shape[0],), jnp.float32)
    upper = jnp.max(scores, axis=1) + 1.0

    def bisect(step, state):
        low, high = state
        middle = 0.5 * (low + high)
        counted = jnp.sum((scores >= middle[:, None]).astype(jnp.int32), axis=1)
        rising = counted >= ranks
        return (jnp.where(rising, middle, low), jnp.where(rising, high, middle))

    lower, upper = lax.fori_loop(0, 24, bisect, (lower, upper))
    start = jnp.min(jnp.where(scores >= lower[:, None], scores, jnp.inf), axis=1)

    def strictly_above(candidate):
        return jnp.sum((scores > candidate[:, None]).astype(jnp.int32), axis=1)

    def unfinished(candidate):
        return jnp.any(strictly_above(candidate) >= ranks)

    def advance(candidate):
        further = strictly_above(candidate) >= ranks
        following = jnp.min(jnp.where(scores > candidate[:, None], scores, jnp.inf), axis=1)
        return jnp.where(further, following, candidate)

    return lax.while_loop(unfinished, advance, start)


def clipped(scores, limits):
    return jnp.maximum(scores - limits[:, None], 0.0)


def per_device(attn_in, attn_out, valid, w_qkv, w_out, qkv_ranks, out_ranks):
    weight = valid.astype(jnp.float32)[:, None]

    def squares(acts):
        acts32 = acts.astype(jnp.float32)
        return jnp.sum(acts32 * acts32 * weight, axis=0)

    partial_sums = jnp.stack([squares(attn_in), squares(attn_out)])
    total_tokens = attn_in.shape[0] * lax.axis_size("seq") * lax.axis_size("rows")
    seq_index = lax.axis_index("seq")
    totals = lax.psum(partial_sums, ("seq", "rows"))
    full_norm = jnp.sqrt(totals / total_tokens + EPS)
    qkv_whole, out_whole = (
        lax.all_to_all(w_qkv, "seq", split_axis=0, concat_axis=1, tiled=True),
        lax.all_to_all(w_out, "seq", split_axis=0, concat_axis=1, tiled=True),
    )
    qkv_rows = tile_scores(qkv_whole, full_norm[0])
    out_rows = tile_scores(out_whole, full_norm[1])
    qkv_count = qkv_rows.shape[0]
    out_count = out_rows.shape[0]
    qkv_mine = lax.dynamic_slice_in_dim(qkv_ranks, seq_index * qkv_count, qkv_count)
    out_mine = lax.dynamic_slice_in_dim(out_ranks, seq_index * out_count, out_count)
    qkv_limits = row_limits(qkv_rows, qkv_mine)
    out_limits = row_limits(out_rows, out_mine)
    qkv_result, out_result = (
        lax.all_to_all(
            clipped(qkv_rows, qkv_limits), "seq", split_axis=1, concat_axis=0, tiled=True
        ),
        lax.all_to_all(
            clipped(out_rows, out_limits), "seq", split_axis=1, concat_axis=0, tiled=True
        ),
    )
    return (qkv_result, out_result)


def solution(mesh):
    placed = (
        P(("seq", "rows"), None),
        P(("seq", "rows"), None),
        P(("seq", "rows")),
        P("rows", "seq"),
        P("rows", "seq"),
        P("rows"),
        P("rows"),
    )
    return jax.shard_map(
        per_device,
        mesh=mesh,
        in_specs=placed,
        out_specs=(P("rows", "seq"), P("rows", "seq")),
        check_vma=False,
    )
```

profile of v0, /device:TPU:0, one launch (start us, length us, event | category | flops | bytes accessed | tf_op | source)
XLA Modules:
  0.0 810.4 jit_solution(17134786051954232279)
XLA Ops:
  7.2 7.3 all-to-all-start.2
  14.5 4.7 multiply_reduce_fusion.1
  22.7 165.7 %all-reduce.2.cloned.1.call-done = f32[2,8192]{1,0:T(2,128)} async-done(((f32[2,8192]{1,0:T(2,128)}), f32[2,8192]{1,0:T(2,128)}) %all-reduce.2.cloned.1.call-update) | async-done | bytes 65552 | tf_op jit(solution)/shard_map/psum | solution.py:55
  189.5 5.4 all-to-all-start
  204.4 122.3 %while.43 = (s32[]{:T(128)}, f32[256]{0:T(256)S(1)}, f32[256]{0:T(256)S(1)}, f32[256,8192]{1,0:T(8,128)}, s32[256]{0:T(256)}, /*index=5*/s32[]{:T(128)}, s32[]{:T(128)}) while((s32[]{:T(128)}, f32[256]{0:T(256)S(1)}, f32[256]{0:T(256)S(1)}, f32[256,8192]{1,0:T(8,128)}, s32[256]{0:T(256)}, /*index=5*/s32[]{:T(128)}, ...), condition=%wide.region_17.18_spmd.clone, body=%wide.region_15.17_spmd.clone.sunk | while | flops 6292995 | bytes 8402528 | solution.py:24
  209.5 4.4 convert_reduce_fusion.7
  219.7 4.4 convert_reduce_fusion.7
  229.9 4.4 convert_reduce_fusion.7
  235.0 4.4 convert_reduce_fusion.7
  326.7 4.5 fusion.10
  331.2 6.6 while.39
  337.8 7.1 fusion.11
  344.9 21.1 %all-to-all-start.3 = ((f32[256,8,1024]{2,0,1:T(8,128)}), f32[256,8,1024]{2,0,1:T(8,128)}, u32[]{:S(2)}, u32[]{:S(2)}) async-start(f32[256,8,1024]{2,0,1:T(8,128)} %fusion.11), calls=%async_computation.3 | async-start | bytes 16777216 | tf_op jit(solution)/shard_map/all_to_all | solution.py:73
  370.2 5.2 copy.11
  375.4 9.7 %broadcast_multiply_fusion = f32[320,8192]{1,0:T(8,128)} fusion(f32[320,8192]{1,0:T(8,128)} %bitcast.30, f32[8192]{0:T(1024)S(1)} %bitcast.34), kind=kLoop, calls=%fused_computation.39 | loop fusion | flops 2621440 | bytes 21004288 | tf_op jit(solution)/shard_map/mul | solution.py:10
  385.0 141.9 %while.42 = (s32[]{:T(128)}, f32[320]{0:T(512)S(1)}, f32[320]{0:T(512)S(1)}, f32[320,8192]{1,0:T(8,128)}, s32[320]{0:T(512)}, /*index=5*/s32[]{:T(128)}, s32[]{:T(128)}) while((s32[]{:T(128)}, f32[320]{0:T(512)S(1)}, f32[320]{0:T(512)S(1)}, f32[320,8192]{1,0:T(8,128)}, s32[320]{0:T(512)}, /*index=5*/s32[]{:T(128)}, s32[]{:T(128)}) %tuple.71), condition=%wide.region_6.7_spmd.clone, body=%wide.region_4.6_spmd.clone.sunk | while | flops 7866243 | bytes 10503136 | solution.py:24
  385.0 5.2 convert_reduce_fusion.6
  391.0 5.2 convert_reduce_fusion.6
  396.9 5.2 convert_reduce_fusion.6
  402.8 5.2 convert_reduce_fusion.6
  408.7 5.2 convert_reduce_fusion.6
  414.6 5.2 convert_reduce_fusion.6
  420.5 5.2 convert_reduce_fusion.6
  426.4 5.2 convert_reduce_fusion.6
  432.4 5.2 convert_reduce_fusion.6
  438.3 5.2 convert_reduce_fusion.6
  444.2 5.2 convert_reduce_fusion.6
  450.1 5.2 convert_reduce_fusion.6
  456.0 5.2 convert_reduce_fusion.6
  461.9 5.2 convert_reduce_fusion.6
  467.8 5.2 convert_reduce_fusion.6
  473.7 5.2 convert_reduce_fusion.6
  479.7 5.2 convert_reduce_fusion.6
  485.6 5.2 convert_reduce_fusion.6
  491.5 5.2 convert_reduce_fusion.6
  497.4 5.2 convert_reduce_fusion.6
  503.3 5.2 convert_reduce_fusion.6
  509.2 5.2 convert_reduce_fusion.6
  515.1 5.2 convert_reduce_fusion.6
  521.0 5.2 convert_reduce_fusion.6
  526.9 5.3 fusion.5
  532.2 7.4 while.37
  532.2 5.2 convert_reduce_fusion
  539.6 8.4 %fusion.6 = f32[320,8,1024]{2,0,1:T(8,128)} fusion(bf16[8,320,1024]{2,1,0:T(8,128)(2,1)} %all-to-all-done, f32[320]{0:T(512)} %get-tuple-element.95, f32[8,1024]{1,0:T(8,128)S(1)} %mul.81), kind=kLoop, calls=%fused_computation.25 | loop fusion | flops 13107200 | bytes 15762688 | tf_op jit(solution)/shard_map/max | solution.py:42
  548.1 22.4 %all-to-all-start.1 = ((f32[320,8,1024]{2,0,1:T(8,128)}), f32[320,8,1024]{2,0,1:T(8,128)}, u32[]{:S(2)}, u32[]{:S(2)}) async-start(f32[320,8,1024]{2,0,1:T(8,128)} %fusion.6), calls=%async_computation.1 | async-start | bytes 20971520 | tf_op jit(solution)/shard_map/all_to_all | solution.py:70
  570.5 214.4 %all-to-all-done.1 = f32[320,8,1024]{2,0,1:T(8,128)} async-done(((f32[320,8,1024]{2,0,1:T(8,128)}), f32[320,8,1024]{2,0,1:T(8,128)}, u32[]{:S(2)}, u32[]{:S(2)}) %all-to-all-start.1) | async-done | bytes 10485792 | tf_op jit(solution)/shard_map/all_to_all | solution.py:70
  784.9 10.3 %copy.40 = f32[2560,1024]{1,0:T(8,128)} copy(f32[2560,1024]{1,0:T(8,128)} %bitcast.7) | data formatting | bytes 20971520
  795.2 8.4 %copy.41 = f32[2048,1024]{1,0:T(8,128)} copy(f32[2048,1024]{1,0:T(8,128)} %bitcast.13) | data formatting | bytes 16777216
  (190 shorter events, 146.8 us)
Async XLA Ops:
  7.2 7.4 copy-start.2
  7.2 182.3 %all-to-all-start.2 = ((bf16[8,256,1024]{2,1,0:T(8,128)(2,1)}), bf16[8,256,1024]{2,1,0:T(8,128)(2,1)}, u32[]{:S(2)}, u32[]{:S(2)}) async-start(bf16[8,256,1024]{2,1,0:T(8,128)(2,1)} %bitcast.33), calls=%async_computation.2 | async-start | bytes 8388608 | tf_op jit(solution)/shard_map/all_to_all | solution.py:59
  14.5 173.9 %all-reduce.2.cloned.1.call-start = ((), (), s32[]{:S(2)}) async-start(), calls=%async_computation.4 | async-start | bytes 131072 | tf_op jit(solution)/shard_map/psum | solution.py:55
  189.5 155.4 %all-to-all-start = ((bf16[8,320,1024]{2,1,0:T(8,128)(2,1)}), bf16[8,320,1024]{2,1,0:T(8,128)(2,1)}, u32[]{:S(2)}, u32[]{:S(2)}) async-start(bf16[8,320,1024]{2,1,0:T(8,128)(2,1)} %bitcast.32), calls=%async_computation | async-start | bytes 10485760 | tf_op jit(solution)/shard_map/all_to_all | solution.py:58
  344.9 203.1 %all-to-all-start.3 = ((f32[256,8,1024]{2,0,1:T(8,128)}), f32[256,8,1024]{2,0,1:T(8,128)}, u32[]{:S(2)}, u32[]{:S(2)}) async-start(f32[256,8,1024]{2,0,1:T(8,128)} %fusion.11), calls=%async_computation.3 | async-start | bytes 16777216 | tf_op jit(solution)/shard_map/all_to_all | solution.py:73
  548.1 236.8 %all-to-all-start.1 = ((f32[320,8,1024]{2,0,1:T(8,128)}), f32[320,8,1024]{2,0,1:T(8,128)}, u32[]{:S(2)}, u32[]{:S(2)}) async-start(f32[320,8,1024]{2,0,1:T(8,128)} %fusion.6), calls=%async_computation.1 | async-start | bytes 20971520 | tf_op jit(solution)/shard_map/all_to_all | solution.py:70
Sparse Core Ops, SparseCore 0:
  21.4 166.8 all-reduce.1
where the time goes:
time: 827 us; the launch traced here: 810 us
  waiting for transfers between devices  380 us (46%)
  other arithmetic  329 us (40%)
  starting transfers between devices  56.3 us (7%)
  local copies, waits for them, and re-layouts  28.5 us (3%)
  between operations  14.2 us (2%)
    reduce_sum x48, other arithmetic, bisect(): counted = jnp.sum((scores >= middle[:, None]).astype(jnp.int32), axis=1)  229 us
    all_to_all x1, waiting for transfers between devices, per_device(): lax.all_to_all(clipped(qkv_rows, qkv_limits), 'seq', split_axis=1, concat...  214 us
    psum x1, waiting for transfers between devices, per_device(): totals = lax.psum(partial_sums, ('seq', 'rows'))  166 us
    select_n x96, other arithmetic, bisect(): return (jnp.where(rising, middle, low), jnp.where(rising, high, middle))  33.9 us
    all_to_all x1, starting transfers between devices, per_device(): lax.all_to_all(clipped(qkv_rows, qkv_limits), 'seq', split_axis=1, concat...  22.4 us
    all_to_all x1, starting transfers between devices, per_device(): lax.all_to_all(clipped(out_rows, out_limits), 'seq', split_axis=1, concat...  21.1 us
    unnamed x4, local copies, waits for them, and re-layouts  18.7 us
  transfers between devices with their start and end apart: 5, of which 2 were waited for; matrix products, arithmetic and copies ran while one was open for 42% of the time, Pallas kernels for 0%

commit v1 on v0

v1 whole, which is shorter than its diff:
```python
import functools

import jax
import jax.numpy as jnp
from jax import lax
from jax.experimental import pallas as pl
from jax.experimental.pallas import tpu as pltpu
from jax.sharding import PartitionSpec as P

EPS = 1e-06
LANES = 128
BIG = 3.0e38
MESH = pl.DeviceIdType.MESH
PLAN = ((4, 0.06, 0.0), (4, 3.5, 1.0), (4, 3.0, 1.0), (4, 2.0, 1.0),
        (4, None, 0.0), (4, None, 0.0), (4, None, 0.0))


def search_kernel(
    n_seq, n_rows, cols, tokens, groups, *refs
):
    (part_ref, wq_ref, wo_ref, kq_ref, ko_ref,
     norm_ref, loq_ref, hiq_ref, loo_ref, hio_ref, flag_ref,
     scores, normb, precv, psum, rrecv, probes, entries,
     sendq, sendo, recvq, recvo, flag_mine, flag_recv,
     p_send, p_recv, r_send, r_recv, q_send, q_recv, o_send, o_recv,
     f_send, f_recv) = refs
    me = lax.axis_index("seq")
    my_row = lax.axis_index("rows")
    width = cols * n_seq
    blocks = cols // LANES
    base = float(1 << cols.bit_length())
    w_refs = (wq_ref, wo_ref)
    k_refs = (kq_ref, ko_ref)
    sends = (sendq, sendo)
    recvs = (recvq, recvo)
    s_sems = (q_send, o_send)
    r_sems = (q_recv, o_recv)
    starts = (0, groups[0])
    rounds = len(PLAN)

    def seq_peer(offset):
        return lax.rem(me + offset, n_seq)

    def row_peer(offset):
        return lax.rem(my_row + offset, n_rows)

    barrier = pltpu.get_barrier_semaphore()
    for offset in range(1, n_seq):
        pl.semaphore_signal(barrier, inc=1, device_id={"seq": seq_peer(offset)}, device_id_type=MESH)
    for offset in range(1, n_rows):
        pl.semaphore_signal(barrier, inc=1, device_id={"rows": row_peer(offset)}, device_id_type=MESH)
    pl.semaphore_wait(barrier, n_seq + n_rows - 2)

    def start_all(axis, count, peer_of, mine, source_of, landing, ssem_of, rsem_of):
        copies = []
        for offset in range(1, count):
            peer = peer_of(offset)
            copy = pltpu.make_async_remote_copy(
                src_ref=source_of(peer), dst_ref=landing(mine),
                send_sem=ssem_of(offset), recv_sem=rsem_of(mine),
                device_id={axis: peer}, device_id_type=MESH)
            copy.start()
            copies.append(copy)
        return copies

    def wait_all(axis, count, peer_of, source_of, landing, ssem_of, rsem_of):
        for offset in range(1, count):
            peer = peer_of(offset)
            pltpu.make_async_remote_copy(
                src_ref=source_of(peer), dst_ref=landing(peer),
                send_sem=ssem_of(offset), recv_sem=rsem_of(peer),
                device_id={axis: peer}, device_id_type=MESH).wait_recv()

    pending = []
    p_args = (lambda peer: part_ref.at[peer], lambda slot: precv.at[slot],
              lambda o: p_send.at[o], lambda s: p_recv.at[s])
    pending += start_all("seq", n_seq, seq_peer, me, *p_args)
    precv[me] = part_ref[me]

    for half in range(2):
        def flip(step, carry, half=half):
            g = step // blocks
            c = step % blocks
            row = pl.multiple_of(g * LANES, LANES)
            col = pl.multiple_of(c * LANES, LANES)
            block = w_refs[half][pl.ds(row, LANES), pl.ds(col, LANES)].astype(jnp.float32)
            scores[starts[half] + g, pl.ds(col, LANES), :] = jnp.abs(block).T
            return carry
        lax.fori_loop(0, groups[half] * blocks, flip, 0, unroll=4)

    wait_all("seq", n_seq, seq_peer, *p_args)
    total = precv[0]
    for s in range(1, n_seq):
        total = total + precv[s]
    psum[...] = total
    rrecv[my_row] = total
    r_args = (lambda peer: psum, lambda slot: rrecv.at[slot],
              lambda o: r_send.at[o], lambda s: r_recv.at[s])
    pending += start_all("rows", n_rows, row_peer, my_row, *r_args)
    wait_all("rows", n_rows, row_peer, *r_args)
    total = rrecv[0]
    for s in range(1, n_rows):
        total = total + rrecv[s]
    norm = jnp.sqrt(total / tokens + EPS)
    norm_ref[...] = norm
    for i in range(2 * blocks):
        normb[i] = jnp.broadcast_to(norm[i:i + 1, :], (LANES, LANES)).T

    def fold(values):
        return values.reshape(LANES // 8, 8, LANES)

    def round_args(half, r, words):
        def part(ref):
            return ref.at[pl.ds(0, words)]
        return (lambda peer: part(sends[half].at[r]),
                lambda slot: part(recvs[half].at[r, slot]),
                lambda o: s_sems[half].at[r, o],
                lambda s: r_sems[half].at[r, s])

    def publish(half, r, words):
        out = []
        for w in range(words):
            recvs[half][r, me, w] = sends[half][r, w]
        out = start_all("seq", n_seq, seq_peer, me, *round_args(half, r, words))
        pending.extend(out)

    def collect(half, r, words):
        wait_all("seq", n_seq, seq_peer, *round_args(half, r, words))

    for half in range(2):
        def scale(g, carry, half=half):
            def column(c, acc):
                col = pl.multiple_of(c * LANES, LANES)
                value = scores[starts[half] + g, pl.ds(col, LANES), :] * normb[half * blocks + c]
                scores[starts[half] + g, pl.ds(col, LANES), :] = value
                return acc + jnp.sum(fold(value), axis=0)
            acc = lax.fori_loop(0, blocks, column, jnp.zeros((8, LANES), jnp.float32), unroll=True)
            sends[half][0, 0, pl.ds(g, 1), :] = jnp.sum(acc, axis=0, keepdims=True)
            return carry
        lax.fori_loop(0, groups[half], scale, 0)
        publish(half, 0, 1)

    state = [None, None]

    def spread(half, r):
        count, wide, extra = PLAN[r]
        guess, lo, hi, clo, chi, k = state[half]
        steps = [i - (count - 1) / 2 for i in range(count)]
        if r == 0:
            points = [guess * (1.0 + s * wide * 1.2) for s in steps]
        elif wide is None:
            top = jnp.where(hi > 1.0e38, 2.0 * lo + guess, hi)
            points = [lo + (top - lo) * (0.5 + s / (count + 1)) for s in steps]
        else:
            top = jnp.where(hi > 1.0e38, 2.0 * lo + guess, hi)
            below = clo - k + 0.5
            above = k - 0.5 - chi
            inside = jnp.maximum(clo - chi, 1.0)
            deviation = wide * jnp.sqrt(jnp.maximum(below * above / inside, 0.0)) + extra
            points = [lo + (top - lo) * jnp.clip((below + s * deviation) / inside, 0.02, 0.98)
                      for s in steps]
        for i in range(1, count):
            points[i] = jnp.maximum(points[i], points[i - 1])
        for i in range(count):
            probes[half, i, pl.ds(0, groups[half]), :] = points[i]
        return points

    def count_all(half, r):
        count = PLAN[r][0]
        def group(g, carry):
            limits = [jnp.broadcast_to(probes[half, i, pl.ds(g, 1), :], (LANES, LANES))
                      for i in range(count)]
            def column(c, accs):
                col = pl.multiple_of(c * LANES, LANES)
                value = scores[starts[half] + g, pl.ds(col, LANES), :]
                out = []
                for w in range(count // 2):
                    marked = jnp.where(value >= limits[2 * w + 1], base + 1.0,
                                       jnp.where(value >= limits[2 * w], 1.0, 0.0))
                    out.append(accs[w] + jnp.sum(fold(marked), axis=0))
                return tuple(out)
            zero = jnp.zeros((8, LANES), jnp.float32)
            accs = lax.fori_loop(0, blocks, column, (zero,) * (count // 2), unroll=2)
            for w in range(count // 2):
                sends[half][r + 1, w, pl.ds(g, 1), :] = jnp.sum(accs[w], axis=0, keepdims=True)
            return carry
        lax.fori_loop(0, groups[half], group, 0)

    def narrow(half, r, points):
        count = PLAN[r][0]
        guess, lo, hi, clo, chi, k = state[half]
        for w in range(count // 2):
            lower = jnp.zeros_like(lo)
            upper = jnp.zeros_like(lo)
            for s in range(n_seq):
                word = recvs[half][r + 1, s, w]
                high = jnp.floor(word * (1.0 / base))
                upper = upper + high
                lower = lower + (word - high * base)
            for point, number in ((points[2 * w], lower), (points[2 * w + 1], upper)):
                enough = number >= k
                rise = enough & (point > lo)
                fall = (number < k) & (point < hi)
                lo = jnp.where(rise, point, lo)
                clo = jnp.where(rise, number, clo)
                hi = jnp.where(fall, point, hi)
                chi = jnp.where(fall, number, chi)
        state[half] = (guess, lo, hi, clo, chi, k)

    points = [None, None]
    for r in range(rounds):
        for half in range(2):
            if r == 0:
                collect(half, 0, 1)
                sums = recvs[half][0, 0, 0]
                for s in range(1, n_seq):
                    sums = sums + recvs[half][0, s, 0]
                mean = sums * (1.0 / width)
                k = k_refs[half][...]
                p = k * (1.0 / width) - 0.5
                guess = mean * (0.845 - 1.996 * p + 1.12 * p * p)
                zero = jnp.zeros_like(k)
                state[half] = (guess, zero, zero + BIG, zero + float(width), zero, k)
            else:
                collect(half, r, PLAN[r - 1][0] // 2)
                narrow(half, r - 1, points[half])
            points[half] = spread(half, r)
            count_all(half, r)
            publish(half, r + 1, PLAN[r][0] // 2)

    last = rounds + 1
    for half in range(2):
        collect(half, rounds, PLAN[-1][0] // 2)
        narrow(half, rounds - 1, points[half])
        guess, lo, hi, clo, chi, k = state[half]
        probes[half, 0, pl.ds(0, groups[half]), :] = lo
        probes[half, 1, pl.ds(0, groups[half]), :] = hi
        def ends(g, carry, half=half):
            low = jnp.broadcast_to(probes[half, 0, pl.ds(g, 1), :], (LANES, LANES))
            high = jnp.broadcast_to(probes[half, 1, pl.ds(g, 1), :], (LANES, LANES))
            def column(c, accs):
                col = pl.multiple_of(c * LANES, LANES)
                value = scores[starts[half] + g, pl.ds(col, LANES), :]
                least = jnp.min(fold(jnp.where(value >= low, value, BIG)), axis=0)
                most = jnp.max(fold(jnp.where(value < high, value, -1.0)), axis=0)
                return (jnp.minimum(accs[0], least), jnp.maximum(accs[1], most))
            least, most = lax.fori_loop(
                0, blocks, column,
                (jnp.full((8, LANES), BIG, jnp.float32), jnp.full((8, LANES), -1.0, jnp.float32)),
                unroll=2)
            sends[half][last, 0, pl.ds(g, 1), :] = jnp.min(least, axis=0, keepdims=True)
            sends[half][last, 1, pl.ds(g, 1), :] = jnp.max(most, axis=0, keepdims=True)
            return carry
        lax.fori_loop(0, groups[half], ends, 0)
        publish(half, last, 2)

    open_rows = jnp.zeros((1, LANES), jnp.float32)
    for half in range(2):
        collect(half, last, 2)
        guess, lo, hi, clo, chi, k = state[half]
        span = pl.ds(0, groups[half])
        known = jnp.zeros_like(lo)
        least_all = jnp.full_like(lo, BIG)
        most_all = jnp.full_like(lo, -1.0)
        for s in range(n_seq):
            least = recvs[half][last, s, 0]
            most = recvs[half][last, s, 1]
            least_all = jnp.minimum(least_all, least)
            most_all = jnp.maximum(most_all, most)
            has = least < hi
            two = has & (most > least)
            entries[half, 2 * s, span, :] = jnp.where(has, least, BIG)
            entries[half, 2 * s + 1, span, :] = jnp.where(two, most, BIG)
            known = known + jnp.where(has, 1.0, 0.0) + jnp.where(two, 1.0, 0.0)
        place = clo - k

        def pick(e, found):
            mine = entries[half, e, span, :]
            less = jnp.zeros_like(mine)
            upto = jnp.zeros_like(mine)
            for other in range(2 * n_seq):
                value = entries[half, other, span, :]
                less = less + jnp.where(value < mine, 1.0, 0.0)
                upto = upto + jnp.where(value <= mine, 1.0, 0.0)
            hit = (less <= place) & (upto > place) & (mine < BIG)
            return jnp.where(hit, mine, found)

        found = lax.fori_loop(0, 2 * n_seq, pick, jnp.full_like(lo, -1.0))
        whole = (known == clo - chi) & (found >= 0.0)
        first = clo == k
        final = chi == k - 1.0
        limit = jnp.where(first, least_all, jnp.where(final, most_all, found))
        solved = first | final | whole
        lo_ref, hi_ref = ((loq_ref, hiq_ref), (loo_ref, hio_ref))[half]
        lo_ref[...] = jnp.where(solved, limit, lo)
        hi_ref[...] = jnp.where(solved, limit, hi)
        open_rows = open_rows + jnp.sum(jnp.where(solved, 0.0, 1.0), axis=0, keepdims=True)

    flag_mine[...] = jnp.broadcast_to(open_rows, (8, LANES))
    flag_recv[my_row] = flag_mine[...]
    f_args = (lambda peer: flag_mine, lambda slot: flag_recv.at[slot],
              lambda o: f_send.at[o], lambda s: f_recv.at[s])
    pending += start_all("rows", n_rows, row_peer, my_row, *f_args)
    wait_all("rows", n_rows, row_peer, *f_args)
    total = flag_recv[0]
    for s in range(1, n_rows):
        total = total + flag_recv[s]
    flag_ref[...] = total
    for copy in pending:
        copy.wait_send()


def per_device(attn_in, attn_out, valid, w_qkv, w_out, qkv_ranks, out_ranks):
    n_seq, n_rows = lax.axis_size("seq"), lax.axis_size("rows")
    weight = valid.astype(jnp.float32)[:, None]

    def squares(acts):
        acts32 = acts.astype(jnp.float32)
        return jnp.sum(acts32 * acts32 * weight, axis=0)

    tokens = attn_in.shape[0] * n_seq * n_rows
    cols = w_qkv.shape[1]
    blocks = cols // LANES
    partial = jnp.stack([squares(attn_in), squares(attn_out)])
    partial = partial.reshape(2, n_seq, blocks, LANES).transpose(1, 0, 2, 3)
    partial = partial.reshape(n_seq, 2 * blocks, LANES)
    groups = (w_qkv.shape[0] // LANES, w_out.shape[0] // LANES)
    ranks = [r.astype(jnp.float32).reshape(-1, LANES) for r in (qkv_ranks, out_ranks)]
    steps = len(PLAN) + 2
    most = max(groups)
    vmem = pl.BlockSpec(memory_space=pltpu.VMEM)
    f32 = jnp.float32

    def shape(*dims):
        return jax.ShapeDtypeStruct(dims, f32)

    dma = pltpu.SemaphoreType.DMA
    norm, loq, hiq, loo, hio, flag = pl.pallas_call(
        functools.partial(search_kernel, n_seq, n_rows, cols, tokens, groups),
        out_shape=[shape(2 * blocks, LANES), shape(groups[0], LANES), shape(groups[0], LANES),
                   shape(groups[1], LANES), shape(groups[1], LANES), shape(8, LANES)],
        in_specs=[vmem] * 5,
        out_specs=[vmem] * 6,
        scratch_shapes=[
            pltpu.VMEM((sum(groups), cols, LANES), f32),
            pltpu.VMEM((2 * blocks, LANES, LANES), f32),
            pltpu.VMEM((n_seq, 2 * blocks, LANES), f32),
            pltpu.VMEM((2 * blocks, LANES), f32),
            pltpu.VMEM((n_rows, 2 * blocks, LANES), f32),
            pltpu.VMEM((2, 4, most, LANES), f32),
            pltpu.VMEM((2, 2 * n_seq, most, LANES), f32),
            pltpu.VMEM((steps, 2, groups[0], LANES), f32),
            pltpu.VMEM((steps, 2, groups[1], LANES), f32),
            pltpu.VMEM((steps, n_seq, 2, groups[0], LANES), f32),
            pltpu.VMEM((steps, n_seq, 2, groups[1], LANES), f32),
            pltpu.VMEM((8, LANES), f32),
            pltpu.VMEM((n_rows, 8, LANES), f32),
            dma((n_seq,)), dma((n_seq,)), dma((n_rows,)), dma((n_rows,)),
            dma((steps, n_seq)), dma((steps, n_seq)), dma((steps, n_seq)), dma((steps, n_seq)),
            dma((n_rows,)), dma((n_rows,)),
        ],
        compiler_params=pltpu.CompilerParams(
            collective_id=0, has_side_effects=True, vmem_limit_bytes=60 * 1024 * 1024),
        name="search",
    )(partial, w_qkv, w_out, *ranks)
    norm = norm.reshape(2, cols)

    def scored(weights, row):
        return jnp.abs(weights.astype(f32)) * norm[row][None, :]

    def going(state):
        return state[0] > 0.0

    def halve(state):
        unused, bounds = state
        results = []
        active = jnp.float32(0.0)
        for row, (weights, ranked) in enumerate(((w_qkv, qkv_ranks), (w_out, out_ranks))):
            low, high = bounds[2 * row], bounds[2 * row + 1]
            middle = 0.5 * (low + high)
            counted = jnp.sum((scored(weights, row) >= middle[:, None]).astype(f32), axis=1)
            counted = lax.psum(counted, "seq")
            rising = counted >= ranked.astype(f32)
            moving = (middle > low) & (middle < high)
            results.append(jnp.where(moving & rising, middle, low))
            results.append(jnp.where(moving & ~rising, middle, high))
            active = jnp.maximum(active, jnp.max(moving.astype(f32)))
        return (lax.psum(active, ("seq", "rows")), tuple(results))

    start = (flag[0].sum(), tuple(x.reshape(-1) for x in (loq, hiq, loo, hio)))
    unused, bounds = lax.while_loop(going, halve, start)
    return (
        jnp.maximum(scored(w_qkv, 0) - bounds[0][:, None], 0.0),
        jnp.maximum(scored(w_out, 1) - bounds[2][:, None], 0.0),
    )


def solution(mesh):
    placed = (
        P(("seq", "rows"), None),
        P(("seq", "rows"), None),
        P(("seq", "rows")),
        P("rows", "seq"),
        P("rows", "seq"),
        P("rows"),
        P("rows"),
    )
    return jax.shard_map(
        per_device,
        mesh=mesh,
        in_specs=placed,
        out_specs=(P("rows", "seq"), P("rows", "seq")),
        check_vma=False,
    )
```

time: 827 us -> 135 us (0.16); the launches traced: 810 us -> 135 us
  waiting for transfers between devices: 380 us -> 0 us
  other arithmetic: 329 us -> 21 us
  Pallas kernels: 0 us -> 111 us
  starting transfers between devices: 56.3 us -> 0 us
  local copies, waits for them, and re-layouts: 28.5 us -> 0.73 us
  between operations: 14.2 us -> 0.7 us
    reduce_sum x50 -> x1, other arithmetic: 239 us -> 1.27 us  [per_device(): flag[0].sum()]
    all_to_all x4 -> x0, waiting for transfers between devices: 214 us -> none  [the longest x1 214 us: per_device(): lax.all_to_all(clipped(qkv_rows, qkv_limits), 'seq', split_axis=1, concat...]
    psum x1 -> x0, waiting for transfers between devices: 166 us -> none  [per_device(): totals = lax.psum(partial_sums, ('seq', 'rows'))]
    pallas_call x0 -> x1, Pallas kernels: none -> 111 us  [per_device(): pl.pallas_call(functools.partial(search_kernel, n_seq, n_rows, cols, toke...]
    all_to_all x4 -> x0, starting transfers between devices: 56.3 us -> none  [the longest x1 22.4 us: per_device(): lax.all_to_all(clipped(qkv_rows, qkv_limits), 'seq', split_axis=1, concat...]
    select_n x96 -> x0, other arithmetic: 33.9 us -> none  [bisect(): return (jnp.where(rising, middle, low), jnp.where(rising, high, middle))]
    unnamed x4 -> x8, local copies, waits for them, and re-layouts: 18.7 us -> 0.02 us
    mul x50 -> x0, other arithmetic: 14.4 us -> none  [the longest x2 14 us: tile_scores(): return jnp.abs(weights.astype(jnp.float32)) * norm[None, :]]
  transfers between devices with their start and end apart: 5 -> 0, of which waited for: 2 -> 0; matrix products, arithmetic and copies ran while one was open for 42% -> 0% of each run, Pallas kernels for 0% -> 0%
where the time goes in v1:
time: 135 us
  Pallas kernels  111 us (82%)
  other arithmetic  21 us (16%)
    pallas_call x1, Pallas kernels, per_device(): pl.pallas_call(functools.partial(search_kernel, n_seq, n_rows, cols, toke...  111 us
    max x1, other arithmetic, per_device(): jnp.maximum(scored(w_qkv, 0) - bounds[0][:, None], 0.0)  8.43 us
    reduce_sum x1, other arithmetic, squares(): return jnp.sum(acts32 * acts32 * weight, axis=0)  4.7 us
    max x1, other arithmetic, per_device(): jnp.maximum(scored(w_out, 1) - bounds[2][:, None], 0.0)  4.09 us

profile of v1, /device:TPU:0, one launch (start us, length us, event | category | flops | bytes accessed | tf_op | source)
XLA Modules:
  0.0 134.5 jit_solution(8545372376933375758)
XLA Ops:
  0.6 0.0 copy-start.2
  0.6 0.0 copy-start.3
  0.7 0.7 convert_element_type.59
  1.3 4.7 %multiply_reduce_fusion.1 = (f32[8192]{0:T(1024)S(1)}, f32[8192]{0:T(1024)S(1)}) fusion(bf16[256,8192]{1,0:T(8,128)(2,1)} %param.9, f32[256]{0:T(256)S(1)} %convert_element_type.59, bf16[256,8192]{1,0:T(8,128)(2,1)} %param.10), kind=kLoop, calls=%fused_computation.21 | loop fusion | flops 16760832 | bytes 8455168 | tf_op jit(solution)/shard_map/reduce_sum | solution.py:319
  6.1 0.6 maximum_bitcast_fusion.refs_0_
  6.7 0.0 copy-done.2
  6.7 0.6 fusion.3
  7.3 0.0 copy-done.3
  7.3 0.6 fusion.4
  7.9 111.2 %search.1 = (f32[16,128]{1,0:T(8,128)}, f32[20,128]{1,0:T(8,128)S(1)}, f32[20,128]{1,0:T(8,128)S(1)}, f32[16,128]{1,0:T(8,128)S(1)}, f32[16,128]{1,0:T(8,128)S(1)}, /*index=5*/f32[8,128]{1,0:T(8,128)}) custom-call(f32[8,16,128]{2,1,0:T(8,128)} %maximum_bitcast_fusion.refs_0_, bf16[2560,1024]{1,0:T(8,128)(2,1)} %refs_1_.1, bf16[2048,1024]{1,0:T(8,128)(2,1)} %refs_2_.1, ...), custom_call_target="tpu_custom_call" | custom-call | tf_op jit(solution)/shard_map/search/pallas_call | solution.py:338
  119.1 0.7 reshape.49
  119.8 1.3 slice_reduce_fusion
  121.1 0.0 copy-start.1
  121.1 0.8 while.18
  122.0 0.0 copy-start
  122.0 0.0 copy-done.1
  122.0 8.4 %subtract_maximum_fusion = f32[2560,1024]{1,0:T(8,128)} fusion(bf16[2560,1024]{1,0:T(8,128)(2,1)} %get-tuple-element.288, f32[2560]{0:T(1024)S(1)} %get-tuple-element.130, f32[1024]{0:T(1024)S(1)} %get-tuple-element.169), kind=kLoop, calls=%fused_computation.18 | loop fusion | flops 13107200 | bytes 15742976 | tf_op jit(solution)/shard_map/max | solution.py:393
  130.4 0.0 copy-done
  130.4 4.1 %subtract_maximum_fusion.1 = f32[2048,1024]{1,0:T(8,128)} fusion(bf16[2048,1024]{1,0:T(8,128)(2,1)S(1)} %copy-done, f32[2048]{0:T(1024)S(1)} %get-tuple-element.131, f32[1024]{0:T(1024)S(1)} %get-tuple-element.168), kind=kLoop, calls=%fused_computation.19 | loop fusion | flops 10485760 | bytes 12595200 | tf_op jit(solution)/shard_map/max | solution.py:394
  (1 shorter events, 0.0 us)
Async XLA Ops:
  0.6 6.1 %copy-start.2 = (s32[2560]{0:T(1024)S(1)}, s32[2560]{0:T(1024)}, u32[]{:S(2)}) copy-start(s32[2560]{0:T(1024)} %param.14) | copy-start | bytes 30724
  0.6 6.7 %copy-start.3 = (s32[2048]{0:T(1024)S(1)}, s32[2048]{0:T(1024)}, u32[]{:S(2)}) copy-start(s32[2048]{0:T(1024)} %param.15) | copy-start | bytes 24580
  121.1 0.9 copy-start.1
  122.0 8.5 %copy-start = (bf16[2048,1024]{1,0:T(8,128)(2,1)S(1)}, bf16[2048,1024]{1,0:T(8,128)(2,1)}, u32[]{:S(2)}) copy-start(bf16[2048,1024]{1,0:T(8,128)(2,1)} %get-tuple-element.289) | copy-start | bytes 12582916
